TPU v7x, 32 devices: a whole 2x2x4 slice. The times are simulated.
32 devices in a mesh: view: 4 (over x, core), depth: 8 (over z, y).
Axes of the slice: x: 2, y: 2, z: 4, core: 2. Of those that a mesh axis runs over, the one named last changes fastest.
Arguments:
- volume: float32 [128, 128, 512], P(('view', 'depth')), may hold values from -6 to 6
- step_weights: float32 [4, 8, 64], P('view'), may hold values from -0.75 to 0.75
- row_interp: float32 [4, 64, 64], P('view'), may hold values from -0.75 to 0.75
- col_interp: float32 [4, 64, 64], P('view'), may hold values from -0.75 to 0.75
- tf_table: float32 [8, 8], replicated, may hold values from -3 to 3
- materials: int32 [2, 2, 8], P(None, None, 'depth'), may hold values from 0 to 7
- entry: int32 [4, 128, 128], P('view'), may hold values from 0 to 3
Outputs:
- picture: float32 [4, 3, 128, 128], P('view', None, 'depth')
All inputs are finite; a program needn't handle non-finite values.
Results may differ from a plain program's by a relative error of at most 0.00018.
Values sent between devices are 32-bit elements; how exact they have to be, the bound alone decides.
No kernel may reach another device: no remote copies, remote signals or barrier semaphores. Data moves between devices by JAX's collectives and lax.ppermute only.
A program may use at most 64 MiB of HBM per device.

v0:
```python
import jax
import jax.numpy as jnp
from jax import lax
from jax.sharding import PartitionSpec as P


def prefix(part, axis, combine, identity):
    place = lax.axis_index(axis)
    gathered = lax.all_gather(part, axis)
    state = jnp.zeros_like(part) + jnp.asarray(identity, part.dtype)

    def one(lap, state):
        return combine(state, lax.dynamic_index_in_dim(gathered, lap, 0, False))

    return lax.fori_loop(0, place, one, state)


def finish_brick(first, rows_map, cols_map):
    highest = lax.Precision.HIGHEST
    edge = rows_map.shape[0]
    count_steps, total_rows, total_cols = first.shape
    second = first.reshape(count_steps, total_rows // edge, edge, total_cols)
    second = jnp.einsum("stky,rk->stry", second, rows_map, precision=highest)
    third = second.reshape(count_steps, total_rows, total_cols // edge, edge)
    third = jnp.einsum("szuj,cj->szuc", third, cols_map, precision=highest)
    return third.reshape(count_steps, total_rows, total_cols)


def expand_classes(classes, tf_table, edge):
    choices_range = jnp.arange(tf_table.shape[0], dtype=jnp.int32)
    onehot = (classes[:, :, None] == choices_range).astype(jnp.float32)
    tiles = jnp.einsum("abm,mc->cab", onehot, tf_table, precision=lax.Precision.HIGHEST)
    count_coef, tiles_rows, tiles_cols = tiles.shape
    spread = jnp.broadcast_to(
        tiles[:, :, None, :, None], (count_coef, tiles_rows, edge, tiles_cols, edge)
    )
    return spread.reshape(count_coef, tiles_rows * edge, tiles_cols * edge)


def shade(samples, coefficients, live_mask, step_length):
    emission = jax.nn.softplus(coefficients[0:3, None] * samples[None] + coefficients[3:6, None])
    tau = (
        step_length
        * live_mask[None]
        * jax.nn.softplus(coefficients[6][None] * samples + coefficients[7][None])
    )
    earlier = jnp.cumsum(tau, axis=0) - tau
    weights = jnp.exp(-earlier) * (1.0 - jnp.exp(-tau))
    colours = jnp.sum(weights[None] * emission, axis=1)
    passed = jnp.exp(-jnp.sum(tau, axis=0))
    return (colours, passed)


def multiply(earlier, later):
    return earlier * later


def shards(volume, step_weights, row_interp, col_interp, tf_table, materials, entry):
    view_count = lax.axis_size("view")
    depth_count = lax.axis_size("depth")
    depth_index = lax.axis_index("depth")
    planes, lateral, span_cells = volume.shape
    brick_edge = span_cells // depth_count
    all_weights = lax.all_gather(step_weights, "view", axis=0, tiled=True)
    count_steps = all_weights.shape[1]
    cells = volume.reshape(planes, lateral, depth_count, brick_edge)
    contracted = jnp.einsum("zybi,gsi->gbszy", cells, all_weights, precision=lax.Precision.HIGHEST)
    contracted = contracted.reshape(view_count * depth_count, count_steps, planes, lateral)
    received = lax.all_to_all(
        contracted, ("view", "depth"), split_axis=0, concat_axis=2, tiled=True
    )
    samples = finish_brick(received[0], row_interp[0], col_interp[0])
    coefficients = expand_classes(materials[:, :, 0], tf_table, brick_edge)
    live_mask = (entry[0] <= depth_index).astype(jnp.float32)
    step_length = 2.0 / (samples.shape[0] * depth_count)
    colours, passed = shade(samples, coefficients, live_mask, step_length)
    before = prefix(passed, "depth", multiply, jnp.ones_like(passed))
    terms = before[None] * colours
    rows_part = lax.psum_scatter(terms, "depth", scatter_dimension=1, tiled=True)
    return rows_part[None]


def solution(mesh):
    placed = (
        P(("view", "depth"), None, None),
        P("view", None, None),
        P("view", None, None),
        P("view", None, None),
        P(),
        P(None, None, "depth"),
        P("view", None, None),
    )
    return jax.shard_map(
        shards,
        mesh=mesh,
        in_specs=placed,
        out_specs=P("view", None, "depth", None),
        check_vma=False,
    )
```

profile of v0, /device:TPU:0, one launch (start us, length us, event | category | flops | bytes accessed | tf_op | source)
XLA Modules:
  0.0 142.9 jit_solution(2641212617554178664)
XLA Ops:
  6.5 0.0 copy-start
  6.5 6.5 %all_gather.7 = f32[4,8,64]{2,1,0:T(8,128)S(1)} all-gather(f32[1,8,64]{2,1,0:T(8,128)} %param.10), channel_id=1, replica_groups=mesh['view'=4,'depth'=8] {'view'}, dimensions={0}, use_global_device_ids=true | all-gather | bytes 10240 | tf_op jit(solution)/shard_map/all_gather | solution.py:64
  13.0 1.5 %copy.50 = f32[4,128,512]{1,2,0:T(8,128)S(1)} copy(f32[4,128,512]{2,1,0:T(8,128)} %param.9) | data formatting | bytes 2097152 | tf_op args[0]
  14.6 0.6 convolution_bitcast_fusion.1
  15.2 0.0 copy-start.3
  15.2 0.0 copy-start.4
  15.2 0.0 copy-start.1
  15.3 0.9 copy.51
  16.1 6.3 %all-to-all-start = ((f32[32,8,4,128]{3,1,2,0:T(8,128)}), f32[32,8,4,128]{3,1,2,0:T(8,128)S(1)}, u32[]{:S(2)}, u32[]{:S(2)}) async-start(f32[32,8,4,128]{3,1,2,0:T(8,128)} %bitcast.10), calls=%async_computation | async-start | bytes 1048576 | tf_op jit(solution)/shard_map/all_to_all | solution.py:69
  22.4 0.0 reduce-scatter.2.cloned.1.call-start
  22.5 0.0 copy-done.3
  22.5 0.0 copy-done.4
  22.5 0.2 convolution_bitcast_fusion.2
  22.7 0.1 fusion.31
  22.8 0.1 copy.59
  22.9 0.1 fusion.30
  22.9 0.1 copy.65
  23.0 0.1 copy.66
  23.1 0.1 broadcast_in_dim.39
  23.2 0.1 broadcast_in_dim.40
  23.3 0.1 broadcast_in_dim.37
  23.4 0.1 broadcast_in_dim.38
  23.4 0.1 copy.61
  23.5 0.0 copy-done.1
  23.6 0.1 copy.48
  23.7 0.1 broadcast_in_dim.41
  23.8 0.1 broadcast_in_dim.42
  23.9 0.1 broadcast_in_dim.43
  24.0 0.1 broadcast_in_dim.44
  24.1 0.2 broadcast_in_dim.46
  24.3 0.2 add.65
  24.5 0.2 broadcast_in_dim.45
  24.7 0.0 copy-start.2
  24.7 0.2 mul.110
  25.0 13.6 %all-to-all-done = f32[32,8,4,128]{3,1,2,0:T(8,128)S(1)} async-done(((f32[32,8,4,128]{3,1,2,0:T(8,128)}), f32[32,8,4,128]{3,1,2,0:T(8,128)S(1)}, u32[]{:S(2)}, u32[]{:S(2)}) %all-to-all-start) | async-done | bytes 524320 | tf_op jit(solution)/shard_map/all_to_all | solution.py:69
  38.6 0.1 copy.52
  38.8 0.0 copy-done.2
  38.8 0.6 convolution_bitcast_fusion
  39.4 0.6 reshape.101
  40.0 0.0 copy-done
  40.0 1.3 fusion.21
  41.4 0.4 multiply_reduce_fusion
  41.8 0.1 copy.55
  41.9 0.2 copy.60
  42.1 0.5 fusion.4
  42.6 0.2 copy.58
  42.8 31.4 %all_gather.8 = f32[8,128,128]{2,1,0:T(8,128)S(1)} all-gather(f32[1,128,128]{2,1,0:T(8,128)S(1)} %copy.55), channel_id=1, replica_groups=mesh['view'=4,'depth'=8] {'depth'}, dimensions={0}, use_global_device_ids=true | all-gather | bytes 589824 | tf_op jit(solution)/shard_map/all_gather | solution.py:9
  74.2 1.0 fusion.1
  75.2 0.7 broadcast_multiply_fusion
  75.9 0.0 reduce-scatter.2.cloned.1.call-update
  75.9 60.1 %reduce-scatter.2.cloned.1.call-done = f32[3,16,128]{2,1,0:T(8,128)} async-done(((f32[3,128,128]{2,1,0:T(8,128)}), f32[3,16,128]{2,1,0:T(8,128)}) %reduce-scatter.2.cloned.1.call-update) | async-done | bytes 24592 | tf_op jit(solution)/shard_map/reduce_scatter | solution.py:79
  (5 shorter events, 0.0 us)
Async XLA Ops:
  6.5 33.5 %copy-start = (f32[1,64,64]{2,1,0:T(8,128)S(1)}, f32[1,64,64]{2,1,0:T(8,128)}, u32[]{:S(2)}) copy-start(f32[1,64,64]{2,1,0:T(8,128)} %param.12) | copy-start | bytes 49156
  15.2 7.2 %copy-start.3 = (f32[8,8]{1,0:T(8,128)S(1)}, f32[8,8]{1,0:T(8,128)}, u32[]{:S(2)}) copy-start(f32[8,8]{1,0:T(8,128)} %param.13) | copy-start | bytes 772
  15.2 7.2 %copy-start.4 = (s32[2,2,1]{1,2,0:T(1,128)S(1)}, s32[2,2,1]{1,2,0:T(1,128)}, u32[]{:S(2)}) copy-start(s32[2,2,1]{1,2,0:T(1,128)} %param.14) | copy-start | bytes 52
  15.2 8.3 %copy-start.1 = (s32[1,128,128]{2,1,0:T(8,128)S(1)}, s32[1,128,128]{2,1,0:T(8,128)}, u32[]{:S(2)}) copy-start(s32[1,128,128]{2,1,0:T(8,128)} %param.15) | copy-start | bytes 196612
  16.1 22.5 %all-to-all-start = ((f32[32,8,4,128]{3,1,2,0:T(8,128)}), f32[32,8,4,128]{3,1,2,0:T(8,128)S(1)}, u32[]{:S(2)}, u32[]{:S(2)}) async-start(f32[32,8,4,128]{3,1,2,0:T(8,128)} %bitcast.10), calls=%async_computation | async-start | bytes 1048576 | tf_op jit(solution)/shard_map/all_to_all | solution.py:69
  22.4 113.6 %reduce-scatter.2.cloned.1.call-start = ((), (), s32[]{:S(2)}) async-start(), calls=%async_computation.2 | async-start | bytes 221184 | tf_op jit(solution)/shard_map/reduce_scatter | solution.py:79
  24.7 14.1 %copy-start.2 = (f32[1,64,64]{2,1,0:T(8,128)S(1)}, f32[1,64,64]{2,1,0:T(8,128)}, u32[]{:S(2)}) copy-start(f32[1,64,64]{2,1,0:T(8,128)} %param.11) | copy-start | bytes 49156
Sparse Core Ops, SparseCore 0:
  76.0 59.9 reduce-scatter.1
where the time goes:
time: 143 us
  waiting for transfers between devices  73.8 us (52%)
  blocking collectives  37.9 us (27%)
  between operations  13.6 us (10%)
  starting transfers between devices  6.33 us (4%)
  local copies, waits for them, and re-layouts  5.89 us (4%)
  matrix products  2.78 us (2%)
  other arithmetic  2.59 us (2%)
    reduce_scatter x1, waiting for transfers between devices, shards(): lax.psum_scatter(terms, 'depth', scatter_dimension=1, tiled=True)  60.1 us
    all_gather x1, blocking collectives, prefix(): gathered = lax.all_gather(part, axis)  31.4 us
    all_to_all x1, waiting for transfers between devices, shards(): lax.all_to_all(contracted, ('view', 'depth'), split_axis=0, concat_axis=2...  13.6 us
    all_gather x1, blocking collectives, shards(): all_weights = lax.all_gather(step_weights, 'view', axis=0, tiled=True)  6.49 us
    all_to_all x1, starting transfers between devices, shards(): lax.all_to_all(contracted, ('view', 'depth'), split_axis=0, concat_axis=2...  6.29 us
  transfers between devices with their start and end apart: 2, of which 2 were waited for; matrix products, arithmetic and copies ran while one was open for 2% of the time, Pallas kernels for 0%

commit v1 on v0

--- a/solution.py
+++ b/solution.py
@@ -66,8 +66,14 @@
     cells = volume.reshape(planes, lateral, depth_count, brick_edge)
     contracted = jnp.einsum("zybi,gsi->gbszy", cells, all_weights, precision=lax.Precision.HIGHEST)
     contracted = contracted.reshape(view_count * depth_count, count_steps, planes, lateral)
-    received = lax.all_to_all(
-        contracted, ("view", "depth"), split_axis=0, concat_axis=2, tiled=True
+    received = jnp.concatenate(
+        lax.all_to_all(
+            jnp.stack(jnp.split(contracted, lax.axis_size(("view", "depth")), axis=0)),
+            ("view", "depth"),
+            0,
+            0,
+        ),
+        axis=2,
     )
     samples = finish_brick(received[0], row_interp[0], col_interp[0])
     coefficients = expand_classes(materials[:, :, 0], tf_table, brick_edge)

time: 143 us -> 161 us (1.13)
  local copies, waits for them, and re-layouts: 5.89 us -> 24.3 us
    unnamed x12 -> x45, local copies, waits for them, and re-layouts: 1.67 us -> 20.3 us
where the time goes in v1:
time: 161 us
  waiting for transfers between devices  73.9 us (46%)
  blocking collectives  37.6 us (23%)
  local copies, waits for them, and re-layouts  24.3 us (15%)
  between operations  13.6 us (8%)
  starting transfers between devices  6.33 us (4%)
  matrix products  2.77 us (2%)
  other arithmetic  2.59 us (2%)
    reduce_scatter x1, waiting for transfers between devices, shards(): lax.psum_scatter(terms, 'depth', scatter_dimension=1, tiled=True)  60.2 us
    all_gather x1, blocking collectives, prefix(): gathered = lax.all_gather(part, axis)  31.4 us
    unnamed x45, local copies, waits for them, and re-layouts  20.3 us
    all_to_all x1, waiting for transfers between devices, shards(): lax.all_to_all(jnp.stack(jnp.split(contracted, lax.axis_size(('view', 'de...  13.6 us
    all_to_all x1, starting transfers between devices, shards(): lax.all_to_all(jnp.stack(jnp.split(contracted, lax.axis_size(('view', 'de...  6.29 us
    all_gather x1, blocking collectives, shards(): all_weights = lax.all_gather(step_weights, 'view', axis=0, tiled=True)  6.24 us
  transfers between devices with their start and end apart: 2, of which 2 were waited for; matrix products, arithmetic and copies ran while one was open for 2% of the time, Pallas kernels for 0%

profile of v1, /device:TPU:0, one launch (start us, length us, event | category | flops | bytes accessed | tf_op | source)
XLA Modules:
  0.0 161.2 jit_solution(16022445522695697004)
XLA Ops:
  6.5 1.6 copy.81
  8.1 6.2 %all_gather.7 = f32[4,8,64]{2,1,0:T(8,128)S(1)} all-gather(f32[1,8,64]{2,1,0:T(8,128)S(1)} %copy-done.3), channel_id=1, replica_groups=mesh['view'=4,'depth'=8] {'view'}, dimensions={0}, use_global_device_ids=true | all-gather | bytes 10240 | tf_op jit(solution)/shard_map/all_gather | solution.py:64
  14.4 0.6 convolution_bitcast_fusion.1
  15.1 0.6 constant_dynamic-update-slice_fusion.31
  15.7 0.6 constant_dynamic-update-slice_fusion.30
  16.3 0.6 constant_dynamic-update-slice_fusion.29
  16.9 0.6 constant_dynamic-update-slice_fusion.28
  17.5 0.6 constant_dynamic-update-slice_fusion.27
  18.1 0.6 constant_dynamic-update-slice_fusion.26
  18.7 0.6 constant_dynamic-update-slice_fusion.25
  19.3 0.6 constant_dynamic-update-slice_fusion.24
  19.9 0.6 constant_dynamic-update-slice_fusion.23
  20.5 0.6 constant_dynamic-update-slice_fusion.22
  21.1 0.6 constant_dynamic-update-slice_fusion.21
  21.7 0.6 constant_dynamic-update-slice_fusion.20
  22.3 0.6 constant_dynamic-update-slice_fusion.19
  22.9 0.6 constant_dynamic-update-slice_fusion.18
  23.5 0.6 constant_dynamic-update-slice_fusion.17
  24.1 0.6 constant_dynamic-update-slice_fusion.16
  24.7 0.6 constant_dynamic-update-slice_fusion.15
  25.3 0.6 constant_dynamic-update-slice_fusion.14
  25.9 0.6 constant_dynamic-update-slice_fusion.13
  26.5 0.6 constant_dynamic-update-slice_fusion.12
  27.1 0.6 constant_dynamic-update-slice_fusion.11
  27.7 0.6 constant_dynamic-update-slice_fusion.10
  28.3 0.6 constant_dynamic-update-slice_fusion.9
  28.9 0.6 constant_dynamic-update-slice_fusion.8
  29.5 0.6 constant_dynamic-update-slice_fusion.7
  30.1 0.6 constant_dynamic-update-slice_fusion.6
  30.7 0.6 constant_dynamic-update-slice_fusion.5
  31.3 0.6 constant_dynamic-update-slice_fusion.4
  31.9 0.6 constant_dynamic-update-slice_fusion.3
  32.5 0.6 constant_dynamic-update-slice_fusion.2
  33.1 0.6 constant_dynamic-update-slice_fusion.1
  33.7 0.6 constant_dynamic-update-slice_fusion
  34.3 6.3 %all-to-all-start = ((f32[32,1,8,4,128]{4,2,3,1,0:T(8,128)}), f32[32,1,8,4,128]{4,2,3,1,0:T(8,128)S(1)}, u32[]{:S(2)}, u32[]{:S(2)}) async-start(f32[32,1,8,4,128]{4,2,3,1,0:T(8,128)} %constant_dynamic-update-slice_fusion), calls=%async_computation | async-start | bytes 1048576 | tf_op jit(solution)/shard_map/all_to_all | solution.py:70
  40.7 0.2 convolution_bitcast_fusion.2
  41.0 0.1 copy.96
  41.2 0.1 copy.97
  41.5 0.1 copy.79
  41.6 0.1 broadcast_in_dim.41
  41.7 0.1 broadcast_in_dim.42
  41.8 0.1 broadcast_in_dim.43
  41.9 0.1 broadcast_in_dim.44
  42.1 0.1 copy.92
  42.2 0.2 broadcast_in_dim.46
  42.4 0.2 add.65
  42.7 0.1 copy.90
  42.8 0.2 broadcast_in_dim.45
  42.9 0.2 mul.110
  43.2 13.6 %all-to-all-done = f32[32,1,8,4,128]{4,2,3,1,0:T(8,128)S(1)} async-done(((f32[32,1,8,4,128]{4,2,3,1,0:T(8,128)}), f32[32,1,8,4,128]{4,2,3,1,0:T(8,128)S(1)}, u32[]{:S(2)}, u32[]{:S(2)}) %all-to-all-start) | async-done | bytes 524320 | tf_op jit(solution)/shard_map/all_to_all | solution.py:70
  56.8 0.1 copy.83
  57.0 0.6 convolution_bitcast_fusion
  57.6 0.6 reshape.104
  58.2 1.3 fusion.21
  59.6 0.4 multiply_reduce_fusion
  60.0 0.1 copy.86
  60.1 31.4 %all_gather.8 = f32[8,128,128]{2,1,0:T(8,128)S(1)} all-gather(f32[1,128,128]{2,1,0:T(8,128)S(1)} %copy.86), channel_id=1, replica_groups=mesh['view'=4,'depth'=8] {'depth'}, dimensions={0}, use_global_device_ids=true | all-gather | bytes 589824 | tf_op jit(solution)/shard_map/all_gather | solution.py:9
  91.5 0.2 copy.91
  91.7 0.5 fusion.4
  92.2 0.2 copy.89
  92.4 1.0 fusion.1
  93.4 0.7 broadcast_multiply_fusion
  94.1 60.2 %reduce-scatter.2.cloned.1.call-done = f32[3,16,128]{2,1,0:T(8,128)} async-done(((f32[3,128,128]{2,1,0:T(8,128)}), f32[3,16,128]{2,1,0:T(8,128)}) %reduce-scatter.2.cloned.1.call-update) | async-done | bytes 24592 | tf_op jit(solution)/shard_map/reduce_scatter | solution.py:85
  (26 shorter events, 0.6 us)
Async XLA Ops:
  6.5 51.7 %copy-start = (f32[1,64,64]{2,1,0:T(8,128)S(1)}, f32[1,64,64]{2,1,0:T(8,128)}, u32[]{:S(2)}) copy-start(f32[1,64,64]{2,1,0:T(8,128)} %param.12) | copy-start | bytes 49156
  6.5 1.6 copy-start.3
  15.1 25.6 %copy-start.4 = (f32[8,8]{1,0:T(8,128)S(1)}, f32[8,8]{1,0:T(8,128)}, u32[]{:S(2)}) copy-start(f32[8,8]{1,0:T(8,128)} %param.13) | copy-start | bytes 772
  15.1 25.6 %copy-start.5 = (s32[2,2,1]{1,2,0:T(1,128)S(1)}, s32[2,2,1]{1,2,0:T(1,128)}, u32[]{:S(2)}) copy-start(s32[2,2,1]{1,2,0:T(1,128)} %param.14) | copy-start | bytes 52
  16.9 24.6 %copy-start.1 = (s32[1,128,128]{2,1,0:T(8,128)S(1)}, s32[1,128,128]{2,1,0:T(8,128)}, u32[]{:S(2)}) copy-start(s32[1,128,128]{2,1,0:T(8,128)} %param.15) | copy-start | bytes 196612
  34.3 22.5 %all-to-all-start = ((f32[32,1,8,4,128]{4,2,3,1,0:T(8,128)}), f32[32,1,8,4,128]{4,2,3,1,0:T(8,128)S(1)}, u32[]{:S(2)}, u32[]{:S(2)}) async-start(f32[32,1,8,4,128]{4,2,3,1,0:T(8,128)} %constant_dynamic-update-slice_fusion), calls=%async_computation | async-start | bytes 1048576 | tf_op jit(solution)/shard_map/all_to_all | solution.py:70
  40.6 113.7 %reduce-scatter.2.cloned.1.call-start = ((), (), s32[]{:S(2)}) async-start(), calls=%async_computation.2 | async-start | bytes 221184 | tf_op jit(solution)/shard_map/reduce_scatter | solution.py:85
  42.9 14.1 %copy-start.2 = (f32[1,64,64]{2,1,0:T(8,128)S(1)}, f32[1,64,64]{2,1,0:T(8,128)}, u32[]{:S(2)}) copy-start(f32[1,64,64]{2,1,0:T(8,128)} %param.11) | copy-start | bytes 49156
Sparse Core Ops, SparseCore 0:
  94.2 60.0 reduce-scatter.1
